TPU v7x, 32 devices: a whole 2x2x4 slice. The times are simulated.
32 devices in a mesh: grp: 16 (over z, x, core), tp: 2 (over y).
Axes of the slice: x: 2, y: 2, z: 4, core: 2. Of those that a mesh axis runs over, the one named last changes fastest.
Arguments:
- memory_rows: bfloat16 [16384, 4096], P('grp', 'tp'), may hold values from -24 to 24, as said below
- norm_gain: float32 [4096], replicated, may hold values from 0.25 to 1.75
- key_weight: bfloat16 [4096, 4096], P(None, 'tp'), may hold values from -0.09375 to 0.09375
- owner_table: int32 [2048], replicated, may hold values from 0 to 2047, as said below
Outputs:
- placed_keys: bfloat16 [16384, 4096], P('grp', 'tp')
Inputs may be any that keep to these rules, and one draw needn't show every extreme that they name: A permutation of the 2048 block numbers. Block b of the input goes to block position owner_table[b], which lies in group owner_table[b] // 128. The 128 blocks of one group go to all 16 groups, exactly 8 blocks to each of them. `memory_rows`: rows have offsets and scales of their own, and features a common pattern.
All inputs are finite; a program needn't handle non-finite values.
Results may differ from a plain program's by a relative error of at most 0.0049.
Values may be sent and summed in bfloat16 or wider, within the bound.
A program may use at most 64 MiB of HBM per device.

v0:
```python
import jax
import jax.numpy as jnp
from jax import lax
from jax.sharding import PartitionSpec as P

BLK_ROWS = 8


EPS = 1e-05


def to_owners(block_rows, owner_table):
    groups = lax.axis_size("grp")
    position = lax.axis_index("grp")
    row_count, col_count = block_rows.shape
    blocks_here = row_count // BLK_ROWS
    capacity = max(1, blocks_here // groups)
    owned_slots = lax.dynamic_slice_in_dim(owner_table, position * blocks_here, blocks_here)
    target = owned_slots // blocks_here
    block_ids = jnp.arange(blocks_here, dtype=jnp.int32)
    earlier = (target[None, :] == target[:, None]) & (block_ids[None, :] < block_ids[:, None])
    rank = jnp.sum(earlier.astype(jnp.int32), axis=1)
    send_slot = target * capacity + rank
    slot_ids = jnp.arange(groups * capacity, dtype=jnp.int32)
    sender = (send_slot[None, :] == slot_ids[:, None]).astype(jnp.bfloat16)
    flattened = block_rows.reshape(blocks_here, BLK_ROWS * col_count)
    outgoing = jnp.dot(sender, flattened, preferred_element_type=jnp.float32).astype(jnp.bfloat16)
    incoming = lax.all_to_all(outgoing, "grp", split_axis=0, concat_axis=0, tiled=True)
    block_total = owner_table.shape[0]
    inverse = (
        jnp.zeros((block_total,), jnp.int32)
        .at[owner_table]
        .set(jnp.arange(block_total, dtype=jnp.int32))
    )
    arriving = lax.dynamic_slice_in_dim(inverse, position * blocks_here, blocks_here)
    anchor_group = arriving // blocks_here
    anchor_column = arriving % blocks_here
    target_table = owner_table.reshape(groups, blocks_here) // blocks_here
    anchor_targets = target_table[anchor_group]
    before = (anchor_targets == position) & (block_ids[None, :] < anchor_column[:, None])
    anchor_rank = jnp.sum(before.astype(jnp.int32), axis=1)
    source_slot = anchor_group * capacity + anchor_rank
    picker = (source_slot[:, None] == slot_ids[None, :]).astype(jnp.bfloat16)
    placed = jnp.dot(picker, incoming, preferred_element_type=jnp.float32).astype(jnp.bfloat16)
    return placed.reshape(row_count, col_count)


def project(memory_rows, norm_gain, key_weight):
    width = norm_gain.shape[0]
    whole_rows = lax.all_gather(memory_rows, "tp", axis=1, tiled=True)
    values = whole_rows.astype(jnp.float32)
    row_mean = jnp.sum(values, axis=1, keepdims=True) / width
    row_var = jnp.sum(values * values, axis=1, keepdims=True) / width - row_mean * row_mean
    normed = ((values - row_mean) * lax.rsqrt(row_var + EPS) * norm_gain[None, :]).astype(
        jnp.bfloat16
    )
    keys = jnp.dot(normed, key_weight, preferred_element_type=jnp.float32)
    return keys.astype(jnp.bfloat16)


def on_device(memory_rows, norm_gain, key_weight, owner_table):
    keys = project(memory_rows, norm_gain, key_weight)
    return to_owners(keys, owner_table)


def solution(mesh):
    in_specs = (P("grp", "tp"), P(), P(None, "tp"), P())
    out_specs = P("grp", "tp")
    return jax.shard_map(
        on_device, mesh=mesh, in_specs=in_specs, out_specs=out_specs, check_vma=False
    )
```

profile of v0, /device:TPU:11, one launch (start us, length us, event | category | flops | bytes accessed | tf_op | source)
XLA Modules:
  0.0 273.4 jit_solution(16602855746114071187)
XLA Ops:
  6.5 0.0 copy-start.2
  6.5 0.0 all-gather.2.cloned.1.call-start
  6.5 0.7 all-gather.2.cloned.1.call-update
  7.3 0.8 and_select_fusion
  8.0 0.2 convert_reduce_fusion.1
  8.2 0.8 multiply_add_fusion
  9.0 104.9 %all-gather.2.cloned.1.call-done = bf16[1024,4096]{1,0:T(8,128)(2,1)} async-done(((bf16[1024,2048]{1,0:T(8,128)(2,1)}), bf16[1024,4096]{1,0:T(8,128)(2,1)}) %all-gather.2.cloned.1.call-update) | async-done | bytes 8388624 | tf_op jit(solution)/shard_map/all_gather | solution.py:50
  113.9 0.0 copy-start
  113.9 6.1 %convert_reduce_fusion = (f32[1024]{0:T(1024)S(1)}, f32[1024]{0:T(1024)S(1)}) fusion(bf16[1024,4096]{1,0:T(8,128)(2,1)} %all-gather.2.cloned.1.call-done), kind=kLoop, calls=%fused_computation.4 | loop fusion | flops 16775168 | bytes 8396800 | tf_op jit(solution)/shard_map/reduce_sum | solution.py:52
  120.0 0.0 copy-done.2
  120.0 0.0 copy-done
  120.0 21.9 %fusion.11 = bf16[1024,2048]{1,0:T(8,128)(2,1)} fusion(bf16[4096,2048]{1,0:T(8,128)(2,1)} %param.6, bf16[1024,4096]{1,0:T(8,128)(2,1)S(1)} %copy-done, f32[4096]{0:T(1024)S(1)} %copy-done.2, f32[1024]{0:T(1024)S(1)} %get-tuple-element.12, f32[1024]{0:T(1024)S(1)} %get-tuple-element.11), kind=kOutput, calls=%fused_computation.17 | convolution fusion | flops 17202937856 | bytes 29384704 | tf_op jit(solution)/shard_map/dot_general | solution.py:57
  141.9 7.4 %reshape.36 = bf16[128,16384]{1,0:T(8,128)(2,1)} reshape(bf16[1024,2048]{1,0:T(8,128)(2,1)} %fusion.11) | data formatting | bytes 8388608 | tf_op jit(solution)/shard_map/reshape | solution.py:26
  149.3 0.0 copy-start.1
  149.3 5.4 %fusion = bf16[16,8,16384]{2,1,0:T(8,128)(2,1)} fusion(bf16[128,16384]{1,0:T(8,128)(2,1)} %reshape.36, s32[128]{0:T(128)S(1)} %multiply_add_fusion), kind=kOutput, calls=%fused_computation.7 | convolution fusion | flops 538984448 | bytes 8389120 | tf_op jit(solution)/shard_map/dot_general | solution.py:27
  154.7 6.5 %all-to-all-start = ((bf16[16,8,16384]{2,1,0:T(8,128)(2,1)}), bf16[16,8,16384]{2,1,0:T(8,128)(2,1)}, u32[]{:S(2)}, u32[]{:S(2)}) async-start(bf16[16,8,16384]{2,1,0:T(8,128)(2,1)} %fusion), calls=%async_computation | async-start | bytes 8388608 | tf_op jit(solution)/shard_map/all_to_all | solution.py:28
  161.2 0.0 copy-done.1
  161.3 8.0 %scatter_custom_fusion = s32[2048]{0:T(1024)S(1)} fusion(s32[2048]{0:T(1024)S(1)} %compare_select_fusion, s32[2048]{0:T(1024)S(1)} %iota.11, s32[]{:T(128)} %constant.54.clone.1), kind=kCustom, calls=%fused_computation.40 | custom fusion | bytes 8196 | tf_op jit(solution)/shard_map/scatter | solution.py:33
  169.3 0.1 and_select_fusion.1
  169.4 0.1 compare_select_fusion.1
  169.5 0.6 gather_fusion
  170.2 0.2 convert_reduce_fusion.2
  170.4 83.4 %all-to-all-done = bf16[16,8,16384]{2,1,0:T(8,128)(2,1)} async-done(((bf16[16,8,16384]{2,1,0:T(8,128)(2,1)}), bf16[16,8,16384]{2,1,0:T(8,128)(2,1)}, u32[]{:S(2)}, u32[]{:S(2)}) %all-to-all-start) | async-done | bytes 4194336 | tf_op jit(solution)/shard_map/all_to_all | solution.py:28
  253.7 5.5 %convolution_convert_fusion = bf16[128,16384]{1,0:T(8,128)(2,1)} fusion(bf16[16,8,16384]{2,1,0:T(8,128)(2,1)} %all-to-all-done, s32[128]{0:T(128)S(1)} %multiply_add_fusion.1), kind=kOutput, calls=%fused_computation.5 | convolution fusion | flops 538984448 | bytes 8389120 | tf_op jit(solution)/shard_map/dot_general | solution.py:44
  259.2 7.4 %reshape.37 = bf16[1024,2048]{1,0:T(8,128)(2,1)} reshape(bf16[128,16384]{1,0:T(8,128)(2,1)} %convolution_convert_fusion) | data formatting | bytes 8388608 | tf_op jit(solution)/shard_map/reshape | solution.py:45
  (6 shorter events, 0.0 us)
Async XLA Ops:
  6.5 113.4 %copy-start.2 = (f32[4096]{0:T(1024)S(1)}, f32[4096]{0:T(1024)}, u32[]{:S(2)}) copy-start(f32[4096]{0:T(1024)} %param.5) | copy-start | bytes 49156
  6.5 107.3 %all-gather.2.cloned.1.call-start = ((), (), s32[]{:S(2)}) async-start(), calls=%async_computation.1 | async-start | bytes 12582912 | tf_op jit(solution)/shard_map/all_gather | solution.py:50
  113.9 6.1 %copy-start = (bf16[1024,4096]{1,0:T(8,128)(2,1)S(1)}, bf16[1024,4096]{1,0:T(8,128)(2,1)}, u32[]{:S(2)}) copy-start(bf16[1024,4096]{1,0:T(8,128)(2,1)} %all-gather.2.cloned.1.call-done) | copy-start | bytes 25165828
  149.3 12.0 %copy-start.1 = (s32[2048]{0:T(1024)S(1)}, s32[2048]{0:T(1024)}, u32[]{:S(2)}) copy-start(s32[2048]{0:T(1024)} %param.7) | copy-start | bytes 24580
  154.7 99.0 %all-to-all-start = ((bf16[16,8,16384]{2,1,0:T(8,128)(2,1)}), bf16[16,8,16384]{2,1,0:T(8,128)(2,1)}, u32[]{:S(2)}, u32[]{:S(2)}) async-start(bf16[16,8,16384]{2,1,0:T(8,128)(2,1)} %fusion), calls=%async_computation | async-start | bytes 8388608 | tf_op jit(solution)/shard_map/all_to_all | solution.py:28
Sparse Core Ops, SparseCore 0:
  8.9 104.9 all-gather.1
where the time goes:
time: 274 us; the launch traced here: 273 us
  waiting for transfers between devices  189 us (69%)
  matrix products  32.8 us (12%)
  local copies, waits for them, and re-layouts  23.5 us (9%)
  between operations  13.5 us (5%)
  other arithmetic  8.19 us (3%)
  starting transfers between devices  6.51 us (2%)
    all_gather x1, waiting for transfers between devices, project(): whole_rows = lax.all_gather(memory_rows, 'tp', axis=1, tiled=True)  105 us
    all_to_all x1, waiting for transfers between devices, to_owners(): lax.all_to_all(outgoing, 'grp', split_axis=0, concat_axis=0, tiled=True)  83.4 us
    dot_general x1, matrix products, project(): keys = jnp.dot(normed, key_weight, preferred_element_type=jnp.float32)  21.9 us
    scatter x1, local copies, waits for them, and re-layouts, to_owners(): inverse = jnp.zeros((block_total,), jnp.int32).at[owner_table].set(jnp.ar...  8.05 us
    reshape x1, local copies, waits for them, and re-layouts, to_owners(): flattened = block_rows.reshape(blocks_here, BLK_ROWS * col_count)  7.41 us
    reshape x1, local copies, waits for them, and re-layouts, to_owners(): return placed.reshape(row_count, col_count)  7.37 us
    all_to_all x1, starting transfers between devices, to_owners(): lax.all_to_all(outgoing, 'grp', split_axis=0, concat_axis=0, tiled=True)  6.51 us
    reduce_sum x1, other arithmetic, project(): row_mean = jnp.sum(values, axis=1, keepdims=True) / width  6.09 us
  transfers between devices with their start and end apart: 2, of which 2 were waited for; matrix products, arithmetic and copies ran while one was open for 4% of the time, Pallas kernels for 0%

commit v1 on v0

v1 whole, which is shorter than its diff:
```python
import functools

import jax
import jax.numpy as jnp
from jax import lax
from jax.experimental import pallas as pl
from jax.experimental.pallas import tpu as pltpu
from jax.sharding import PartitionSpec as P

BLK_ROWS = 8
EPS = 1e-05
CHUNKS = 8
MIB = 1024 * 1024
MESH = pl.DeviceIdType.MESH


def flipped(me, mask, groups):
    out = me
    bit = 1
    while bit < groups:
        out = out + ((mask // bit) % 2) * bit * (1 - 2 * ((me // bit) % 2))
        bit *= 2
    return out


def sort_kernel(groups, table_ref, rows_ref, out_ref, count_ref, sem):
    me = lax.axis_index("grp")
    blocks = rows_ref.shape[0]
    capacity = blocks // groups

    def clear(g, carry):
        count_ref[g] = 0
        return carry

    lax.fori_loop(0, groups, clear, 0)

    def move(b, carry):
        target = table_ref[me * blocks + b] // blocks
        rank = count_ref[target]
        count_ref[target] = rank + 1
        step = groups - 1 - (me ^ target)
        pltpu.make_async_copy(rows_ref.at[b], out_ref.at[step * capacity + rank], sem).start()
        return carry

    lax.fori_loop(0, blocks, move, 0)
    pltpu.make_async_copy(rows_ref, out_ref, sem).wait()


def place_kernel(groups, slot_ref, in_ref, out_ref, sem):
    me = lax.axis_index("grp")
    blocks = in_ref.shape[0]
    capacity = blocks // groups

    def move(i, carry):
        step = i // capacity
        source = me ^ (groups - 1 - step)
        slot = slot_ref[source, i - step * capacity]
        pltpu.make_async_copy(in_ref.at[i], out_ref.at[slot], sem).start()
        return carry

    lax.fori_loop(0, blocks, move, 0)
    pltpu.make_async_copy(in_ref, out_ref, sem).wait()


def main_kernel(
    groups, parts, rows_ref, gain_ref, weight_ref, out_ref,
    mine, others, weight, keys, normed, gains,
    mine_sem, weight_sem, gain_sem, gather_send, gather_recv, key_send, key_recv, self_sem,
):
    me = lax.axis_index("grp")
    part = lax.axis_index("tp")
    row_count, depth = rows_ref.shape
    width = depth * parts
    chunk = row_count // CHUNKS
    per_chunk = groups // CHUNKS
    piece = row_count // groups

    barrier = pltpu.get_barrier_semaphore()
    for j in range(1, parts):
        pl.semaphore_signal(
            barrier, inc=1, device_id={"tp": (part + j) % parts}, device_id_type=MESH
        )

    def greet(mask, carry):
        pl.semaphore_signal(
            barrier, inc=1, device_id={"grp": flipped(me, mask, groups)}, device_id_type=MESH
        )
        return carry

    lax.fori_loop(1, groups, greet, 0)

    def own_copy(c):
        at = pl.ds(c * chunk, chunk)
        return pltpu.make_async_copy(rows_ref.at[at], mine.at[at], mine_sem.at[c])

    def weight_copy(j):
        origin = (part + j) % parts
        return pltpu.make_async_copy(
            weight_ref.at[pl.ds(pl.multiple_of(origin * depth, depth), depth)],
            weight.at[pl.ds(j * depth, depth)],
            weight_sem.at[j],
        )

    def gain_copy(j):
        origin = (part + j) % parts
        return pltpu.make_async_copy(
            gain_ref.at[:, pl.ds(pl.multiple_of(origin * depth, depth), depth)],
            gains.at[:, pl.ds(j * depth, depth)],
            gain_sem.at[j],
        )

    def gather_copy(c, j):
        at = pl.ds(c * chunk, chunk)
        return pltpu.make_async_remote_copy(
            src_ref=rows_ref.at[at],
            dst_ref=others.at[j - 1, at],
            send_sem=gather_send.at[j - 1, c],
            recv_sem=gather_recv.at[j - 1, c],
            device_id={"tp": (part + parts - j) % parts},
            device_id_type=MESH,
        )

    def key_copy(step):
        at = pl.ds(step * piece, piece)
        return pltpu.make_async_remote_copy(
            src_ref=keys.at[at],
            dst_ref=out_ref.at[at],
            send_sem=key_send.at[step],
            recv_sem=key_recv.at[step],
            device_id={"grp": flipped(me, groups - 1 - step, groups)},
            device_id_type=MESH,
        )

    def self_copy():
        at = pl.ds((groups - 1) * piece, piece)
        return pltpu.make_async_copy(keys.at[at], out_ref.at[at], self_sem)

    for j in range(parts):
        gain_copy(j).start()
        weight_copy(j).start()
    for c in range(CHUNKS):
        own_copy(c).start()
    pl.semaphore_wait(barrier, groups - 1 + parts - 1)
    for c in range(CHUNKS):
        for j in range(1, parts):
            gather_copy(c, j).start()
    for j in range(parts):
        gain_copy(j).wait()
        weight_copy(j).wait()

    sub = 2 * BLK_ROWS
    tile = depth // 4

    def one_chunk(c, carry):
        base = pl.multiple_of(c * chunk, chunk)
        own_copy(c).wait()
        for j in range(1, parts):
            gather_copy(c, j).wait_recv()

        def norm_rows(i, carry):
            at = pl.ds(pl.multiple_of(base + i * sub, sub), sub)
            to = pl.ds(pl.multiple_of(i * sub, sub), sub)

            def values(j):
                held = mine[at, :] if j == 0 else others[j - 1, at, :]
                return held.astype(jnp.float32)

            row_sum = 0.0
            row_sq = 0.0
            for j in range(parts):
                x = values(j)
                row_sum = row_sum + jnp.sum(x, axis=1, keepdims=True)
                row_sq = row_sq + jnp.sum(x * x, axis=1, keepdims=True)
            mean = row_sum / width
            scale = lax.rsqrt(row_sq / width - mean * mean + EPS)
            for j in range(parts):
                cols = pl.ds(j * depth, depth)
                normed[to, cols] = ((values(j) - mean) * scale * gains[:, cols]).astype(
                    jnp.bfloat16
                )
            return carry

        lax.fori_loop(0, chunk // sub, norm_rows, 0)

        def columns(n, carry):
            cols = pl.ds(pl.multiple_of(n * tile, tile), tile)
            keys[pl.ds(base, chunk), cols] = jnp.dot(
                normed[...], weight[:, cols], preferred_element_type=jnp.float32
            ).astype(jnp.bfloat16)
            return carry

        lax.fori_loop(0, keys.shape[1] // tile, columns, 0)

        for i in range(per_chunk):
            step = c * per_chunk + i
            if i < per_chunk - 1:
                key_copy(step).start()
            else:
                @pl.when(c < CHUNKS - 1)
                def _():
                    key_copy(step).start()

                @pl.when(c == CHUNKS - 1)
                def _():
                    self_copy().start()
        return carry

    lax.fori_loop(0, CHUNKS, one_chunk, 0)

    for c in range(CHUNKS):
        for j in range(1, parts):
            gather_copy(c, j).wait_send()

    def finish(step, carry):
        key_copy(step).wait()
        return carry

    lax.fori_loop(0, groups - 1, finish, 0)
    self_copy().wait()


def on_device(groups, parts, memory_rows, norm_gain, key_weight, owner_table):
    row_count, depth = memory_rows.shape
    columns = key_weight.shape[1]
    blocks = row_count // BLK_ROWS
    capacity = blocks // groups
    position = lax.axis_index("grp")
    any_space = pl.BlockSpec(memory_space=pl.ANY)
    in_vmem = pl.BlockSpec(memory_space=pltpu.VMEM)
    in_smem = pl.BlockSpec(memory_space=pltpu.SMEM)

    in_order = pl.pallas_call(
        functools.partial(sort_kernel, groups),
        out_shape=jax.ShapeDtypeStruct((blocks, BLK_ROWS, depth), jnp.bfloat16),
        in_specs=[in_smem, any_space],
        out_specs=in_vmem,
        scratch_shapes=[pltpu.SMEM((groups,), jnp.int32), pltpu.SemaphoreType.DMA],
        compiler_params=pltpu.CompilerParams(vmem_limit_bytes=16 * MIB),
        name="sort",
    )(owner_table, memory_rows.reshape(blocks, BLK_ROWS, depth))

    table = owner_table.reshape(groups, blocks)
    to_me = table // blocks == position
    lower = jnp.triu(jnp.ones((blocks, blocks), jnp.bfloat16), 1)
    rank = jnp.dot(to_me.astype(jnp.bfloat16), lower, preferred_element_type=jnp.float32)
    rank = jnp.where(to_me, rank.astype(jnp.int32), -1)
    wanted = jnp.arange(capacity, dtype=jnp.int32)[None, :, None]
    slots = jnp.sum(jnp.where(rank[:, None, :] == wanted, (table % blocks)[:, None, :], 0), axis=2)

    dma = pltpu.SemaphoreType.DMA
    incoming = pl.pallas_call(
        functools.partial(main_kernel, groups, parts),
        out_shape=jax.ShapeDtypeStruct((row_count, columns), jnp.bfloat16),
        in_specs=[any_space, any_space, any_space],
        out_specs=any_space,
        scratch_shapes=[
            pltpu.VMEM((row_count, depth), jnp.bfloat16),
            pltpu.VMEM((parts - 1, row_count, depth), jnp.bfloat16),
            pltpu.VMEM((depth * parts, columns), jnp.bfloat16),
            pltpu.VMEM((row_count, columns), jnp.bfloat16),
            pltpu.VMEM((row_count // CHUNKS, depth * parts), jnp.bfloat16),
            pltpu.VMEM((1, depth * parts), jnp.float32),
            dma((CHUNKS,)),
            dma((parts,)),
            dma((parts,)),
            dma((parts - 1, CHUNKS)),
            dma((parts - 1, CHUNKS)),
            dma((groups,)),
            dma((groups,)),
            dma,
        ],
        compiler_params=pltpu.CompilerParams(
            collective_id=0, has_side_effects=True, vmem_limit_bytes=48 * MIB
        ),
        name="exchange",
    )(in_order.reshape(row_count, depth), norm_gain[None, :], key_weight)

    placed = pl.pallas_call(
        functools.partial(place_kernel, groups),
        out_shape=jax.ShapeDtypeStruct((blocks, BLK_ROWS, columns), jnp.bfloat16),
        in_specs=[in_smem, in_vmem],
        out_specs=any_space,
        scratch_shapes=[pltpu.SemaphoreType.DMA],
        compiler_params=pltpu.CompilerParams(vmem_limit_bytes=16 * MIB),
        name="place",
    )(slots, incoming.reshape(blocks, BLK_ROWS, columns))
    return placed.reshape(row_count, columns)


def solution(mesh):
    in_specs = (P("grp", "tp"), P(), P(None, "tp"), P())
    out_specs = P("grp", "tp")
    return jax.shard_map(
        functools.partial(on_device, mesh.shape["grp"], mesh.shape["tp"]),
        mesh=mesh, in_specs=in_specs, out_specs=out_specs, check_vma=False,
    )
```

time: 274 us -> 143 us (0.52)
  the two profiles are of different devices: /device:TPU:11 before, /device:TPU:0 now
where the time goes in v1:
time: 143 us
  Pallas kernels  136 us (95%)
  local copies, waits for them, and re-layouts  4.89 us (3%)
    pallas_call x1, Pallas kernels, on_device(): pl.pallas_call(functools.partial(main_kernel, groups, parts), out_shape=j...  124 us
    pallas_call x1, Pallas kernels, on_device(): pl.pallas_call(functools.partial(sort_kernel, groups), out_shape=jax.Shap...  8.6 us
    unnamed x8, local copies, waits for them, and re-layouts  4.89 us
    pallas_call x1, Pallas kernels, on_device(): pl.pallas_call(functools.partial(place_kernel, groups), out_shape=jax.Sha...  3.12 us

profile of v1, /device:TPU:0, one launch (start us, length us, event | category | flops | bytes accessed | tf_op | source)
XLA Modules:
  0.0 142.9 jit_solution(11996925773621477424)
XLA Ops:
  0.0 0.9 fusion
  0.9 0.7 add_select_fusion
  1.6 0.3 select_reduce_fusion.slot_ref
  2.0 0.0 copy-start.1
  2.0 2.2 %copy-done.1 = bf16[1024,2048]{1,0:T(8,128)(2,1)S(1)} copy-done((bf16[1024,2048]{1,0:T(8,128)(2,1)S(1)}, bf16[1024,2048]{1,0:T(8,128)(2,1)}, u32[]{:S(2)}) %copy-start.1) | copy-done | bytes 4194328
  4.2 0.0 copy-start.2
  4.2 0.7 copy-done.2
  4.9 0.0 copy-start.3
  4.9 8.6 %sort.1 = bf16[128,8,2048]{2,1,0:T(8,128)(2,1)S(1)} custom-call(s32[2048]{0:T(1024)S(1)} %copy-done.2, bf16[128,8,2048]{2,1,0:T(8,128)(2,1)S(1)} %bitcast.49), custom_call_target="tpu_custom_call" | custom-call | tf_op jit(solution)/shard_map/sort/pallas_call | solution.py:232
  13.5 0.0 copy-start
  13.5 2.0 %copy-done = bf16[128,8,2048]{2,1,0:T(8,128)(2,1)} copy-done((bf16[128,8,2048]{2,1,0:T(8,128)(2,1)}, bf16[128,8,2048]{2,1,0:T(8,128)(2,1)S(1)}, u32[]{:S(2)}) %copy-start) | copy-done | bytes 4194328
  15.5 0.0 copy-done.3
  15.5 124.3 %exchange.1 = bf16[1024,2048]{1,0:T(8,128)(2,1)S(1)} custom-call(bf16[1024,2048]{1,0:T(8,128)(2,1)} %bitcast.48, f32[1,4096]{1,0:T(1,128)S(1)} %bitcast.50, bf16[4096,2048]{1,0:T(8,128)(2,1)} %weight_ref.1), custom_call_target="tpu_custom_call" | custom-call | tf_op jit(solution)/shard_map/exchange/pallas_call | solution.py:251
  139.8 3.1 %place.1 = bf16[128,8,2048]{2,1,0:T(8,128)(2,1)} custom-call(s32[16,8]{1,0:T(8,128)S(1)} %select_reduce_fusion.slot_ref, bf16[128,8,2048]{2,1,0:T(8,128)(2,1)S(1)} %bitcast.47), custom_call_target="tpu_custom_call" | custom-call | tf_op jit(solution)/shard_map/place/pallas_call | solution.py:278
Async XLA Ops:
  2.0 2.2 %copy-start.1 = (bf16[1024,2048]{1,0:T(8,128)(2,1)S(1)}, bf16[1024,2048]{1,0:T(8,128)(2,1)}, u32[]{:S(2)}) copy-start(bf16[1024,2048]{1,0:T(8,128)(2,1)} %param.4) | copy-start | bytes 12582916
  4.2 0.7 copy-start.2
  4.9 10.6 %copy-start.3 = (f32[4096]{0:T(1024)S(1)}, f32[4096]{0:T(1024)}, u32[]{:S(2)}) copy-start(f32[4096]{0:T(1024)} %param.5) | copy-start | bytes 49156
  13.5 2.0 %copy-start = (bf16[128,8,2048]{2,1,0:T(8,128)(2,1)}, bf16[128,8,2048]{2,1,0:T(8,128)(2,1)S(1)}, u32[]{:S(2)}) copy-start(bf16[128,8,2048]{2,1,0:T(8,128)(2,1)S(1)} %sort.1) | copy-start | bytes 12582916

commit v2 on v1

--- a/solution.py
+++ b/solution.py
@@ -9,7 +9,7 @@
 
 BLK_ROWS = 8
 EPS = 1e-05
-CHUNKS = 8
+CHUNKS = 16
 MIB = 1024 * 1024
 MESH = pl.DeviceIdType.MESH
 
@@ -23,27 +23,15 @@
     return out
 
 
-def sort_kernel(groups, table_ref, rows_ref, out_ref, count_ref, sem):
-    me = lax.axis_index("grp")
-    blocks = rows_ref.shape[0]
-    capacity = blocks // groups
-
-    def clear(g, carry):
-        count_ref[g] = 0
-        return carry
-
-    lax.fori_loop(0, groups, clear, 0)
-
-    def move(b, carry):
-        target = table_ref[me * blocks + b] // blocks
-        rank = count_ref[target]
-        count_ref[target] = rank + 1
-        step = groups - 1 - (me ^ target)
-        pltpu.make_async_copy(rows_ref.at[b], out_ref.at[step * capacity + rank], sem).start()
-        return carry
-
-    lax.fori_loop(0, blocks, move, 0)
-    pltpu.make_async_copy(rows_ref, out_ref, sem).wait()
+def mask_at(me, step, groups):
+    quarter = groups // 4
+    inner = ((me // quarter + 1) // 2) % 2
+    turn = step // quarter
+    first = (3 - turn) // 3
+    second = (turn % 2) * (1 - turn // 2)
+    third = (turn // 2) * (1 - turn % 2)
+    far = first * (1 + inner) + 3 * second + third * (2 - inner)
+    return far * quarter + quarter - 1 - step % quarter
 
 
 def place_kernel(groups, slot_ref, in_ref, out_ref, sem):
@@ -52,9 +40,8 @@
     capacity = blocks // groups
 
     def move(i, carry):
-        step = i // capacity
-        source = me ^ (groups - 1 - step)
-        slot = slot_ref[source, i - step * capacity]
+        mask = i // capacity
+        slot = slot_ref[me ^ mask, i - mask * capacity]
         pltpu.make_async_copy(in_ref.at[i], out_ref.at[slot], sem).start()
         return carry
 
@@ -63,15 +50,18 @@
 
 
 def main_kernel(
-    groups, parts, rows_ref, gain_ref, weight_ref, out_ref,
-    mine, others, weight, keys, normed, gains,
-    mine_sem, weight_sem, gain_sem, gather_send, gather_recv, key_send, key_recv, self_sem,
+    groups, parts, index_ref, rows_ref, gain_ref, weight_ref, out_ref,
+    raw, mine, others, weight, keys, normed, gains,
+    raw_sem, weight_sem, gain_sem, gather_send, gather_recv, key_send, key_recv, self_sem,
 ):
     me = lax.axis_index("grp")
     part = lax.axis_index("tp")
-    row_count, depth = rows_ref.shape
+    blocks, _, depth = rows_ref.shape
+    row_count = blocks * BLK_ROWS
     width = depth * parts
     chunk = row_count // CHUNKS
+    chunk_blocks = blocks // CHUNKS
+    capacity = blocks // groups
     per_chunk = groups // CHUNKS
     piece = row_count // groups
 
@@ -89,9 +79,7 @@
 
     lax.fori_loop(1, groups, greet, 0)
 
-    def own_copy(c):
-        at = pl.ds(c * chunk, chunk)
-        return pltpu.make_async_copy(rows_ref.at[at], mine.at[at], mine_sem.at[c])
+    raw_copy = pltpu.make_async_copy(rows_ref, raw, raw_sem)
 
     def weight_copy(j):
         origin = (part + j) % parts
@@ -110,9 +98,9 @@
         )
 
     def gather_copy(c, j):
-        at = pl.ds(c * chunk, chunk)
+        at = pl.ds(c * chunk_blocks, chunk_blocks)
         return pltpu.make_async_remote_copy(
-            src_ref=rows_ref.at[at],
+            src_ref=mine.at[at],
             dst_ref=others.at[j - 1, at],
             send_sem=gather_send.at[j - 1, c],
             recv_sem=gather_recv.at[j - 1, c],
@@ -121,27 +109,39 @@
         )
 
     def key_copy(step):
-        at = pl.ds(step * piece, piece)
+        mask = mask_at(me, step, groups)
         return pltpu.make_async_remote_copy(
-            src_ref=keys.at[at],
-            dst_ref=out_ref.at[at],
+            src_ref=keys.at[pl.ds(step * piece, piece)],
+            dst_ref=out_ref.at[pl.ds(mask * piece, piece)],
             send_sem=key_send.at[step],
-            recv_sem=key_recv.at[step],
-            device_id={"grp": flipped(me, groups - 1 - step, groups)},
+            recv_sem=key_recv.at[mask],
+            device_id={"grp": flipped(me, mask, groups)},
             device_id_type=MESH,
         )
 
     def self_copy():
         at = pl.ds((groups - 1) * piece, piece)
-        return pltpu.make_async_copy(keys.at[at], out_ref.at[at], self_sem)
-
+        return pltpu.make_async_copy(keys.at[at], out_ref.at[pl.ds(0, piece)], self_sem)
+
+    raw_copy.start()
     for j in range(parts):
         gain_copy(j).start()
         weight_copy(j).start()
-    for c in range(CHUNKS):
-        own_copy(c).start()
+    raw_copy.wait()
+
+    def arrange(c):
+        def take(i, carry):
+            step = i // capacity
+            mine[i] = raw[index_ref[groups + step, i - step * capacity]]
+            return carry
+
+        lax.fori_loop(c * chunk_blocks, (c + 1) * chunk_blocks, take, 0)
+
+    arrange(0)
     pl.semaphore_wait(barrier, groups - 1 + parts - 1)
     for c in range(CHUNKS):
+        if c > 0:
+            arrange(c)
         for j in range(1, parts):
             gather_copy(c, j).start()
     for j in range(parts):
@@ -153,17 +153,16 @@
 
     def one_chunk(c, carry):
         base = pl.multiple_of(c * chunk, chunk)
-        own_copy(c).wait()
         for j in range(1, parts):
             gather_copy(c, j).wait_recv()
 
         def norm_rows(i, carry):
-            at = pl.ds(pl.multiple_of(base + i * sub, sub), sub)
+            at = pl.ds(c * chunk_blocks + i * 2, 2)
             to = pl.ds(pl.multiple_of(i * sub, sub), sub)
 
             def values(j):
-                held = mine[at, :] if j == 0 else others[j - 1, at, :]
-                return held.astype(jnp.float32)
+                held = mine[at] if j == 0 else others[j - 1, at]
+                return held.astype(jnp.float32).reshape(sub, depth)
 
             row_sum = 0.0
             row_sq = 0.0
@@ -229,38 +228,34 @@
     in_vmem = pl.BlockSpec(memory_space=pltpu.VMEM)
     in_smem = pl.BlockSpec(memory_space=pltpu.SMEM)
 
-    in_order = pl.pallas_call(
-        functools.partial(sort_kernel, groups),
-        out_shape=jax.ShapeDtypeStruct((blocks, BLK_ROWS, depth), jnp.bfloat16),
-        in_specs=[in_smem, any_space],
-        out_specs=in_vmem,
-        scratch_shapes=[pltpu.SMEM((groups,), jnp.int32), pltpu.SemaphoreType.DMA],
-        compiler_params=pltpu.CompilerParams(vmem_limit_bytes=16 * MIB),
-        name="sort",
-    )(owner_table, memory_rows.reshape(blocks, BLK_ROWS, depth))
-
     table = owner_table.reshape(groups, blocks)
-    to_me = table // blocks == position
+    own = lax.dynamic_slice_in_dim(table, position, 1, axis=0)
+    steps = jnp.arange(groups, dtype=jnp.int32)
+    peers = position ^ mask_at(position, steps, groups)
+    chosen = jnp.concatenate([table // blocks == position, own // blocks == peers[:, None]])
+    block_ids = jnp.broadcast_to(jnp.arange(blocks, dtype=jnp.int32)[None], table.shape)
+    values = jnp.concatenate([table % blocks, block_ids])
     lower = jnp.triu(jnp.ones((blocks, blocks), jnp.bfloat16), 1)
-    rank = jnp.dot(to_me.astype(jnp.bfloat16), lower, preferred_element_type=jnp.float32)
-    rank = jnp.where(to_me, rank.astype(jnp.int32), -1)
+    rank = jnp.dot(chosen.astype(jnp.bfloat16), lower, preferred_element_type=jnp.float32)
+    rank = jnp.where(chosen, rank.astype(jnp.int32), -1)
     wanted = jnp.arange(capacity, dtype=jnp.int32)[None, :, None]
-    slots = jnp.sum(jnp.where(rank[:, None, :] == wanted, (table % blocks)[:, None, :], 0), axis=2)
+    index = jnp.sum(jnp.where(rank[:, None, :] == wanted, values[:, None, :], 0), axis=2)
 
     dma = pltpu.SemaphoreType.DMA
     incoming = pl.pallas_call(
         functools.partial(main_kernel, groups, parts),
         out_shape=jax.ShapeDtypeStruct((row_count, columns), jnp.bfloat16),
-        in_specs=[any_space, any_space, any_space],
+        in_specs=[in_smem, any_space, any_space, any_space],
         out_specs=any_space,
         scratch_shapes=[
-            pltpu.VMEM((row_count, depth), jnp.bfloat16),
-            pltpu.VMEM((parts - 1, row_count, depth), jnp.bfloat16),
+            pltpu.VMEM((blocks, BLK_ROWS, depth), jnp.bfloat16),
+            pltpu.VMEM((blocks, BLK_ROWS, depth), jnp.bfloat16),
+            pltpu.VMEM((parts - 1, blocks, BLK_ROWS, depth), jnp.bfloat16),
             pltpu.VMEM((depth * parts, columns), jnp.bfloat16),
             pltpu.VMEM((row_count, columns), jnp.bfloat16),
             pltpu.VMEM((row_count // CHUNKS, depth * parts), jnp.bfloat16),
             pltpu.VMEM((1, depth * parts), jnp.float32),
-            dma((CHUNKS,)),
+            dma,
             dma((parts,)),
             dma((parts,)),
             dma((parts - 1, CHUNKS)),
@@ -273,7 +268,7 @@
             collective_id=0, has_side_effects=True, vmem_limit_bytes=48 * MIB
         ),
         name="exchange",
-    )(in_order.reshape(row_count, depth), norm_gain[None, :], key_weight)
+    )(index, memory_rows.reshape(blocks, BLK_ROWS, depth), norm_gain[None, :], key_weight)
 
     placed = pl.pallas_call(
         functools.partial(place_kernel, groups),
@@ -283,7 +278,7 @@
         scratch_shapes=[pltpu.SemaphoreType.DMA],
         compiler_params=pltpu.CompilerParams(vmem_limit_bytes=16 * MIB),
         name="place",
-    )(slots, incoming.reshape(blocks, BLK_ROWS, columns))
+    )(index, incoming.reshape(blocks, BLK_ROWS, columns))
     return placed.reshape(row_count, columns)
 
 

time: 143 us -> 116 us (0.81)
  the two profiles are of different devices: /device:TPU:0 before, /device:TPU:16 now
where the time goes in v2:
time: 116 us
  Pallas kernels  112 us (97%)
  other arithmetic  2.83 us (2%)
    pallas_call x1, Pallas kernels, on_device(): pl.pallas_call(functools.partial(main_kernel, groups, parts), out_shape=j...  109 us
    pallas_call x1, Pallas kernels, on_device(): pl.pallas_call(functools.partial(place_kernel, groups), out_shape=jax.Sha...  3.25 us

profile of v2, /device:TPU:16, one launch (start us, length us, event | category | flops | bytes accessed | tf_op | source)
XLA Modules:
  0.0 115.6 jit_solution(16501958358256904768)
XLA Ops:
  0.0 0.7 fusion.13
  0.7 0.8 fusion.8
  1.5 0.7 add_select_fusion
  2.2 0.1 fusion
  2.3 0.6 select_reduce_fusion.index_ref.slot_ref
  3.0 0.0 copy-start
  3.0 0.7 copy-done
  3.7 108.6 %exchange.1 = bf16[1024,2048]{1,0:T(8,128)(2,1)S(1)} custom-call(s32[32,8]{1,0:T(8,128)S(1)} %select_reduce_fusion.index_ref.slot_ref, bf16[128,8,2048]{2,1,0:T(8,128)(2,1)} %bitcast.11, f32[1,4096]{1,0:T(1,128)S(1)} %bitcast.10, bf16[4096,2048]{1,0:T(8,128)(2,1)} %weight_ref.1), custom_call_target="tpu_custom_call" | custom-call | tf_op jit(solution)/shard_map/exchange/pallas_call | solution.py:245
  112.3 3.3 %place.1 = bf16[128,8,2048]{2,1,0:T(8,128)(2,1)} custom-call(s32[32,8]{1,0:T(8,128)S(1)} %select_reduce_fusion.index_ref.slot_ref, bf16[128,8,2048]{2,1,0:T(8,128)(2,1)S(1)} %bitcast.9), custom_call_target="tpu_custom_call" | custom-call | tf_op jit(solution)/shard_map/place/pallas_call | solution.py:273
  (3 shorter events, 0.0 us)
Async XLA Ops:
  3.0 0.7 copy-start

commit v3 on v2

--- a/solution.py
+++ b/solution.py
@@ -34,6 +34,47 @@
     return far * quarter + quarter - 1 - step % quarter
 
 
+def peer_mask(me, step, groups, early):
+    regular = groups - early
+    split = groups // 2 - early
+    is_early = step // regular
+    after = (1 + step // split) // 2
+    late = step - regular + split
+    return mask_at(me, is_early * late + (1 - is_early) * (step + early * after), groups)
+
+
+def index_kernel(groups, per_chunk, table_ref, slot_ref, index_ref):
+    me = lax.axis_index("grp")
+    blocks = table_ref.shape[1]
+    capacity = blocks // groups
+
+    lane = lax.broadcasted_iota(jnp.int32, (groups, blocks), 1)
+    row = lax.broadcasted_iota(jnp.int32, (groups, blocks), 0)
+    peer = jnp.zeros((groups, blocks), jnp.int32)
+    for step in range(groups):
+        mask = peer_mask(me, step, groups, per_chunk)
+        peer = jnp.where(row == step, flipped(me, mask, groups), peer)
+
+    def ranked(offset, value):
+        chosen = (offset >= 0) & (offset < blocks)
+        counted = chosen.astype(jnp.int32)
+        shift = 1
+        while shift < blocks:
+            counted = counted + jnp.where(lane >= shift, pltpu.roll(counted, shift, 1), 0)
+            shift *= 2
+        result = jnp.zeros((groups, blocks), jnp.int32)
+        for r in range(capacity):
+            at_rank = jnp.where(chosen & (counted == r + 1), value, 0).astype(jnp.float32)
+            found = jnp.sum(at_rank, axis=1, keepdims=True).astype(jnp.int32)
+            result = jnp.where(lane == r, found, result)
+        return result
+
+    own = jnp.broadcast_to(table_ref[pl.ds(me, 1), :], (groups, blocks))
+    index_ref[...] = ranked(own - peer * blocks, lane)
+    offset = table_ref[...] - me * blocks
+    slot_ref[...] = ranked(offset, offset)
+
+
 def place_kernel(groups, slot_ref, in_ref, out_ref, sem):
     me = lax.axis_index("grp")
     blocks = in_ref.shape[0]
@@ -51,8 +92,8 @@
 
 def main_kernel(
     groups, parts, index_ref, rows_ref, gain_ref, weight_ref, out_ref,
-    raw, mine, others, weight, keys, normed, gains,
-    raw_sem, weight_sem, gain_sem, gather_send, gather_recv, key_send, key_recv, self_sem,
+    raw, away, mine, others, weight, keys, normed, gains,
+    raw_sem, early_send, early_recv, weight_sem, gain_sem, gather_send, gather_recv, key_send, key_recv, self_sem,
 ):
     me = lax.axis_index("grp")
     part = lax.axis_index("tp")
@@ -64,6 +105,7 @@
     capacity = blocks // groups
     per_chunk = groups // CHUNKS
     piece = row_count // groups
+    regular = groups - per_chunk
 
     barrier = pltpu.get_barrier_semaphore()
     for j in range(1, parts):
@@ -109,7 +151,7 @@
         )
 
     def key_copy(step):
-        mask = mask_at(me, step, groups)
+        mask = peer_mask(me, step, groups, per_chunk)
         return pltpu.make_async_remote_copy(
             src_ref=keys.at[pl.ds(step * piece, piece)],
             dst_ref=out_ref.at[pl.ds(mask * piece, piece)],
@@ -119,27 +161,52 @@
             device_id_type=MESH,
         )
 
-    def self_copy():
-        at = pl.ds((groups - 1) * piece, piece)
-        return pltpu.make_async_copy(keys.at[at], out_ref.at[pl.ds(0, piece)], self_sem)
+    def local_copy(i):
+        step = regular + i if i < per_chunk else regular - 1
+        mask = peer_mask(me, step, groups, per_chunk)
+        return pltpu.make_async_copy(
+            keys.at[pl.ds(step * piece, piece)],
+            out_ref.at[pl.ds(mask * piece, piece)],
+            self_sem.at[i],
+        )
+
+    def early_copy(i):
+        mask = peer_mask(me, regular + i, groups, per_chunk)
+        return pltpu.make_async_remote_copy(
+            src_ref=away.at[pl.ds(i * capacity, capacity)],
+            dst_ref=mine.at[pl.ds((regular + i) * capacity, capacity)],
+            send_sem=early_send.at[i],
+            recv_sem=early_recv.at[i],
+            device_id={"grp": flipped(me, mask, groups)},
+            device_id_type=MESH,
+        )
 
     raw_copy.start()
+
     for j in range(parts):
         gain_copy(j).start()
+    raw_copy.wait()
+    for j in range(parts):
         weight_copy(j).start()
-    raw_copy.wait()
 
     def arrange(c):
         def take(i, carry):
             step = i // capacity
-            mine[i] = raw[index_ref[groups + step, i - step * capacity]]
+            block = raw[index_ref[step, i - step * capacity]]
+            if c == CHUNKS - 1:
+                away[i - c * chunk_blocks] = block
+            else:
+                mine[i] = block
             return carry
 
         lax.fori_loop(c * chunk_blocks, (c + 1) * chunk_blocks, take, 0)
 
+    arrange(CHUNKS - 1)
     arrange(0)
     pl.semaphore_wait(barrier, groups - 1 + parts - 1)
-    for c in range(CHUNKS):
+    for i in range(per_chunk):
+        early_copy(i).start()
+    for c in range(CHUNKS - 1):
         if c > 0:
             arrange(c)
         for j in range(1, parts):
@@ -153,6 +220,14 @@
 
     def one_chunk(c, carry):
         base = pl.multiple_of(c * chunk, chunk)
+
+        @pl.when(c == CHUNKS // 2)
+        def _():
+            for i in range(per_chunk):
+                early_copy(i).wait_recv()
+            for j in range(1, parts):
+                gather_copy(CHUNKS - 1, j).start()
+
         for j in range(1, parts):
             gather_copy(c, j).wait_recv()
 
@@ -192,20 +267,23 @@
 
         for i in range(per_chunk):
             step = c * per_chunk + i
-            if i < per_chunk - 1:
+
+            @pl.when(step < regular - 1)
+            def _():
                 key_copy(step).start()
-            else:
-                @pl.when(c < CHUNKS - 1)
-                def _():
-                    key_copy(step).start()
-
-                @pl.when(c == CHUNKS - 1)
-                def _():
-                    self_copy().start()
+
+        @pl.when(c == CHUNKS - 2)
+        def _():
+            local_copy(per_chunk).start()
+
         return carry
 
     lax.fori_loop(0, CHUNKS, one_chunk, 0)
 
+    for i in range(per_chunk):
+        local_copy(i).start()
+    for i in range(per_chunk):
+        early_copy(i).wait_send()
     for c in range(CHUNKS):
         for j in range(1, parts):
             gather_copy(c, j).wait_send()
@@ -214,8 +292,9 @@
         key_copy(step).wait()
         return carry
 
-    lax.fori_loop(0, groups - 1, finish, 0)
-    self_copy().wait()
+    lax.fori_loop(0, regular - 1, finish, 0)
+    for i in range(per_chunk + 1):
+        local_copy(i).wait()
 
 
 def on_device(groups, parts, memory_rows, norm_gain, key_weight, owner_table):
@@ -223,25 +302,21 @@
     columns = key_weight.shape[1]
     blocks = row_count // BLK_ROWS
     capacity = blocks // groups
-    position = lax.axis_index("grp")
     any_space = pl.BlockSpec(memory_space=pl.ANY)
     in_vmem = pl.BlockSpec(memory_space=pltpu.VMEM)
     in_smem = pl.BlockSpec(memory_space=pltpu.SMEM)
 
-    table = owner_table.reshape(groups, blocks)
-    own = lax.dynamic_slice_in_dim(table, position, 1, axis=0)
-    steps = jnp.arange(groups, dtype=jnp.int32)
-    peers = position ^ mask_at(position, steps, groups)
-    chosen = jnp.concatenate([table // blocks == position, own // blocks == peers[:, None]])
-    block_ids = jnp.broadcast_to(jnp.arange(blocks, dtype=jnp.int32)[None], table.shape)
-    values = jnp.concatenate([table % blocks, block_ids])
-    lower = jnp.triu(jnp.ones((blocks, blocks), jnp.bfloat16), 1)
-    rank = jnp.dot(chosen.astype(jnp.bfloat16), lower, preferred_element_type=jnp.float32)
-    rank = jnp.where(chosen, rank.astype(jnp.int32), -1)
-    wanted = jnp.arange(capacity, dtype=jnp.int32)[None, :, None]
-    index = jnp.sum(jnp.where(rank[:, None, :] == wanted, values[:, None, :], 0), axis=2)
-
     dma = pltpu.SemaphoreType.DMA
+    listing = jax.ShapeDtypeStruct((groups, blocks), jnp.int32)
+    slots, index = pl.pallas_call(
+        functools.partial(index_kernel, groups, groups // CHUNKS),
+        out_shape=[listing, listing],
+        in_specs=[in_vmem],
+        out_specs=[in_vmem, in_vmem],
+        compiler_params=pltpu.CompilerParams(vmem_limit_bytes=4 * MIB),
+        name="index",
+    )(owner_table.reshape(groups, blocks))
+
     incoming = pl.pallas_call(
         functools.partial(main_kernel, groups, parts),
         out_shape=jax.ShapeDtypeStruct((row_count, columns), jnp.bfloat16),
@@ -249,6 +324,7 @@
         out_specs=any_space,
         scratch_shapes=[
             pltpu.VMEM((blocks, BLK_ROWS, depth), jnp.bfloat16),
+            pltpu.VMEM((blocks // CHUNKS, BLK_ROWS, depth), jnp.bfloat16),
             pltpu.VMEM((blocks, BLK_ROWS, depth), jnp.bfloat16),
             pltpu.VMEM((parts - 1, blocks, BLK_ROWS, depth), jnp.bfloat16),
             pltpu.VMEM((depth * parts, columns), jnp.bfloat16),
@@ -256,13 +332,15 @@
             pltpu.VMEM((row_count // CHUNKS, depth * parts), jnp.bfloat16),
             pltpu.VMEM((1, depth * parts), jnp.float32),
             dma,
+            dma((groups // CHUNKS,)),
+            dma((groups // CHUNKS,)),
             dma((parts,)),
             dma((parts,)),
             dma((parts - 1, CHUNKS)),
             dma((parts - 1, CHUNKS)),
             dma((groups,)),
             dma((groups,)),
-            dma,
+            dma((groups // CHUNKS + 1,)),
         ],
         compiler_params=pltpu.CompilerParams(
             collective_id=0, has_side_effects=True, vmem_limit_bytes=48 * MIB
@@ -278,7 +356,7 @@
         scratch_shapes=[pltpu.SemaphoreType.DMA],
         compiler_params=pltpu.CompilerParams(vmem_limit_bytes=16 * MIB),
         name="place",
-    )(index, incoming.reshape(blocks, BLK_ROWS, columns))
+    )(slots, incoming.reshape(blocks, BLK_ROWS, columns))
     return placed.reshape(row_count, columns)
 
 

time: 116 us -> 111 us (0.957)
  the two profiles are of different devices: /device:TPU:16 before, /device:TPU:0 now
where the time goes in v3:
time: 111 us; the launch traced here: 110 us
  Pallas kernels  109 us (98%)
  local copies, waits for them, and re-layouts  1.41 us (1%)
    pallas_call x1, Pallas kernels, on_device(): pl.pallas_call(functools.partial(main_kernel, groups, parts), out_shape=j...  105 us
    pallas_call x1, Pallas kernels, on_device(): pl.pallas_call(functools.partial(place_kernel, groups), out_shape=jax.Sha...  3.12 us

profile of v3, /device:TPU:0, one launch (start us, length us, event | category | flops | bytes accessed | tf_op | source)
XLA Modules:
  0.0 110.5 jit_solution(6314445126483413517)
XLA Ops:
  0.0 0.0 copy-start.1
  0.0 0.7 copy-done.1
  0.7 0.7 index.1
  1.4 0.0 copy-start
  1.4 0.7 copy-done
  2.1 105.2 %exchange.1 = bf16[1024,2048]{1,0:T(8,128)(2,1)S(1)} custom-call(s32[16,128]{1,0:T(8,128)S(1)} %get-tuple-element.8.index_ref, bf16[128,8,2048]{2,1,0:T(8,128)(2,1)} %bitcast.8, f32[1,4096]{1,0:T(1,128)S(1)} %bitcast.6, bf16[4096,2048]{1,0:T(8,128)(2,1)} %weight_ref.1), custom_call_target="tpu_custom_call" | custom-call | tf_op jit(solution)/shard_map/exchange/pallas_call | solution.py:320
  107.4 3.1 %place.1 = bf16[128,8,2048]{2,1,0:T(8,128)(2,1)} custom-call(s32[16,128]{1,0:T(8,128)S(1)} %get-tuple-element.7.slot_ref, bf16[128,8,2048]{2,1,0:T(8,128)(2,1)S(1)} %bitcast.5), custom_call_target="tpu_custom_call" | custom-call | tf_op jit(solution)/shard_map/place/pallas_call | solution.py:351
Async XLA Ops:
  0.0 0.7 copy-start.1
  1.4 0.7 copy-start

commit v4 on v3

--- a/solution.py
+++ b/solution.py
@@ -86,7 +86,7 @@
         pltpu.make_async_copy(in_ref.at[i], out_ref.at[slot], sem).start()
         return carry
 
-    lax.fori_loop(0, blocks, move, 0)
+    lax.fori_loop(0, blocks, move, 0, unroll=8)
     pltpu.make_async_copy(in_ref, out_ref, sem).wait()
 
 
@@ -108,18 +108,18 @@
     regular = groups - per_chunk
 
     barrier = pltpu.get_barrier_semaphore()
+    def greet(i, carry):
+        mask = groups - i
+        pl.semaphore_signal(
+            barrier, inc=1, device_id={"grp": flipped(me, mask, groups)}, device_id_type=MESH
+        )
+        return carry
+
+    lax.fori_loop(1, groups, greet, 0)
     for j in range(1, parts):
         pl.semaphore_signal(
             barrier, inc=1, device_id={"tp": (part + j) % parts}, device_id_type=MESH
         )
-
-    def greet(mask, carry):
-        pl.semaphore_signal(
-            barrier, inc=1, device_id={"grp": flipped(me, mask, groups)}, device_id_type=MESH
-        )
-        return carry
-
-    lax.fori_loop(1, groups, greet, 0)
 
     raw_copy = pltpu.make_async_copy(rows_ref, raw, raw_sem)
 
@@ -216,7 +216,7 @@
         weight_copy(j).wait()
 
     sub = 2 * BLK_ROWS
-    tile = depth // 4
+    tile = depth // 2
 
     def one_chunk(c, carry):
         base = pl.multiple_of(c * chunk, chunk)
@@ -303,6 +303,7 @@
     blocks = row_count // BLK_ROWS
     capacity = blocks // groups
     any_space = pl.BlockSpec(memory_space=pl.ANY)
+    in_hbm = pl.BlockSpec(memory_space=pltpu.HBM)
     in_vmem = pl.BlockSpec(memory_space=pltpu.VMEM)
     in_smem = pl.BlockSpec(memory_space=pltpu.SMEM)
 
@@ -320,7 +321,7 @@
     incoming = pl.pallas_call(
         functools.partial(main_kernel, groups, parts),
         out_shape=jax.ShapeDtypeStruct((row_count, columns), jnp.bfloat16),
-        in_specs=[in_smem, any_space, any_space, any_space],
+        in_specs=[in_smem, in_hbm, in_hbm, in_hbm],
         out_specs=any_space,
         scratch_shapes=[
             pltpu.VMEM((blocks, BLK_ROWS, depth), jnp.bfloat16),

time: 111 us -> 109 us (0.982)
  no operation moved by 1% of the time
where the time goes in v4:
time: 109 us
  Pallas kernels  108 us (99%)
  local copies, waits for them, and re-layouts  1.41 us (1%)
    pallas_call x1, Pallas kernels, on_device(): pl.pallas_call(functools.partial(main_kernel, groups, parts), out_shape=j...  104 us
    pallas_call x1, Pallas kernels, on_device(): pl.pallas_call(functools.partial(place_kernel, groups), out_shape=jax.Sha...  2.65 us

profile of v4, /device:TPU:0, one launch (start us, length us, event | category | flops | bytes accessed | tf_op | source)
XLA Modules:
  0.0 109.0 jit_solution(17432915473166270408)
XLA Ops:
  0.0 0.0 copy-start.1
  0.0 0.7 copy-done.1
  0.7 0.7 index.1
  1.4 0.0 copy-start
  1.4 0.7 copy-done
  2.1 104.2 %exchange.1 = bf16[1024,2048]{1,0:T(8,128)(2,1)S(1)} custom-call(s32[16,128]{1,0:T(8,128)S(1)} %get-tuple-element.8.index_ref, bf16[128,8,2048]{2,1,0:T(8,128)(2,1)} %bitcast.8, f32[1,4096]{1,0:T(1,128)S(1)} %bitcast.6, bf16[4096,2048]{1,0:T(8,128)(2,1)} %weight_ref.1), custom_call_target="tpu_custom_call" | custom-call | tf_op jit(solution)/shard_map/exchange/pallas_call | solution.py:321
  106.3 2.6 %place.1 = bf16[128,8,2048]{2,1,0:T(8,128)(2,1)} custom-call(s32[16,128]{1,0:T(8,128)S(1)} %get-tuple-element.7.slot_ref, bf16[128,8,2048]{2,1,0:T(8,128)(2,1)S(1)} %bitcast.5), custom_call_target="tpu_custom_call" | custom-call | tf_op jit(solution)/shard_map/place/pallas_call | solution.py:352
Async XLA Ops:
  0.0 0.7 copy-start.1
  1.4 0.7 copy-start

commit v5 on v4

--- a/solution.py
+++ b/solution.py
@@ -199,24 +199,25 @@
                 mine[i] = block
             return carry
 
-        lax.fori_loop(c * chunk_blocks, (c + 1) * chunk_blocks, take, 0)
-
-    arrange(CHUNKS - 1)
+        lax.fori_loop(c * chunk_blocks, (c + 1) * chunk_blocks, take, 0, unroll=2)
+
     arrange(0)
     pl.semaphore_wait(barrier, groups - 1 + parts - 1)
-    for i in range(per_chunk):
-        early_copy(i).start()
     for c in range(CHUNKS - 1):
         if c > 0:
             arrange(c)
         for j in range(1, parts):
             gather_copy(c, j).start()
+        if c == 0:
+            arrange(CHUNKS - 1)
+            for i in range(per_chunk):
+                early_copy(i).start()
     for j in range(parts):
         gain_copy(j).wait()
         weight_copy(j).wait()
 
     sub = 2 * BLK_ROWS
-    tile = depth // 2
+    tile = depth
 
     def one_chunk(c, carry):
         base = pl.multiple_of(c * chunk, chunk)

time: 109 us -> 109 us (level)
  no operation moved by 1% of the time
where the time goes in v5:
time: 109 us
  Pallas kernels  107 us (98%)
  local copies, waits for them, and re-layouts  1.41 us (1%)
    pallas_call x1, Pallas kernels, on_device(): pl.pallas_call(functools.partial(main_kernel, groups, parts), out_shape=j...  104 us
    pallas_call x1, Pallas kernels, on_device(): pl.pallas_call(functools.partial(place_kernel, groups), out_shape=jax.Sha...  2.65 us

profile of v5, /device:TPU:0, one launch (start us, length us, event | category | flops | bytes accessed | tf_op | source)
XLA Modules:
  0.0 108.8 jit_solution(6932618381239002100)
XLA Ops:
  0.0 0.0 copy-start.1
  0.0 0.7 copy-done.1
  0.7 0.7 index.1
  1.4 0.0 copy-start
  1.4 0.7 copy-done
  2.1 104.1 %exchange.1 = bf16[1024,2048]{1,0:T(8,128)(2,1)S(1)} custom-call(s32[16,128]{1,0:T(8,128)S(1)} %get-tuple-element.8.index_ref, bf16[128,8,2048]{2,1,0:T(8,128)(2,1)} %bitcast.8, f32[1,4096]{1,0:T(1,128)S(1)} %bitcast.6, bf16[4096,2048]{1,0:T(8,128)(2,1)} %weight_ref.1), custom_call_target="tpu_custom_call" | custom-call | tf_op jit(solution)/shard_map/exchange/pallas_call | solution.py:322
  106.2 2.6 %place.1 = bf16[128,8,2048]{2,1,0:T(8,128)(2,1)} custom-call(s32[16,128]{1,0:T(8,128)S(1)} %get-tuple-element.7.slot_ref, bf16[128,8,2048]{2,1,0:T(8,128)(2,1)S(1)} %bitcast.5), custom_call_target="tpu_custom_call" | custom-call | tf_op jit(solution)/shard_map/place/pallas_call | solution.py:353
Async XLA Ops:
  0.0 0.7 copy-start.1
  1.4 0.7 copy-start
